TPU v7x, 32 devices: a whole 2x2x4 slice. The times are simulated.
32 devices in a mesh: seg: 16 (over z, y, x), slab: 2 (over core).
Axes of the slice: x: 2, y: 2, z: 4, core: 2. Of those that a mesh axis runs over, the one named last changes fastest.
Arguments:
- block: float32 [16, 4, 16, 4096], P('seg', None, 'slab'), may hold values from -6 to 6
- base_velocity: bfloat16 [16, 8, 2, 16, 4096], P('seg', None, None, 'slab'), may hold values from -6 to 6
Outputs:
- new_block: float32 [16, 4, 16, 4096], P('seg', None, 'slab')
All inputs are finite; a program needn't handle non-finite values.
Results may differ from a plain program's by a relative error of at most 0.0003.
Values may be sent and summed in bfloat16 or wider, within the bound.
No kernel may reach another device: no remote copies, remote signals or barrier semaphores. Data moves between devices by JAX's collectives and lax.ppermute only.
A program may use at most 64 MiB of HBM per device.

v0:
```python
import jax
import jax.numpy as jnp
from jax import lax
from jax.sharding import PartitionSpec as P

HOPS = 4


def with_halo(shard, sides, width):
    for axis, dim in sides:
        size, length = (lax.axis_size(axis), shard.shape[dim])
        up = [(i, (i + 1) % size) for i in range(size)]
        down = [(j, i) for i, j in up]
        last = lax.slice_in_dim(shard, length - width, length, axis=dim)
        first = lax.slice_in_dim(shard, 0, width, axis=dim)
        before = lax.ppermute(last, axis, up)
        after = lax.ppermute(first, axis, down)
        shard = jnp.concatenate([before, shard, after], axis=dim)
    return shard


def shifted(block, axis, distance):
    devices = range(lax.axis_size(axis))
    route = [((i - distance) % len(devices), i) for i in devices]
    return lax.ppermute(block, axis, route)


def advance(padded, velocity):
    centre = padded[:, 1:-1]
    up = padded[:, 2:]
    down = padded[:, :-2]
    east = jnp.roll(centre, -1, 2)
    west = jnp.roll(centre, 1, 2)
    speed_x = velocity[0].astype(jnp.float32)
    speed_y = velocity[1].astype(jnp.float32)
    return (
        centre
        + 0.2 * (up + down + east + west - 4.0 * centre)
        - 0.05 * (speed_x * (east - west) + speed_y * (up - down))
        - 0.02 * centre
    )


def lower_inverse(lower):
    count = lower.shape[0]
    rows = []
    for i in range(count):
        entries = []
        for j in range(count):
            if j > i:
                entries.append(jnp.zeros((), jnp.float32))
            elif j == i:
                entries.append(1.0 / lower[i, i])
            else:
                total = jnp.zeros((), jnp.float32)
                for k in range(j, i):
                    total = total + lower[i, k] * rows[k][j]
                entries.append(-total / lower[i, i])
        rows.append(entries)
    return jnp.stack([jnp.stack(r) for r in rows])


def shards(block, base_velocity):
    vectors = block[0]
    velocity = base_velocity[0]
    depth = velocity.shape[0]
    velocity_wide = with_halo(velocity, (("slab", 2),), depth)
    for hop in range(HOPS):
        moved = with_halo(vectors, (("slab", 1),), depth)
        for j in range(depth):
            height = velocity_wide.shape[2]
            moved = advance(moved, velocity_wide[j][:, j + 1 : height - j - 1])
        arrived = shifted(moved, "seg", 1)
        residual = arrived - vectors
        local_gram = jnp.einsum("ayx,byx->ab", residual, residual, precision=lax.Precision.HIGHEST)
        gram = lax.psum(local_gram, ("seg", "slab"))
        inverse = lower_inverse(jnp.linalg.cholesky(gram))
        vectors = jnp.einsum("ab,byx->ayx", inverse, residual, precision=lax.Precision.HIGHEST)
    return vectors[None]


def solution(mesh):
    placed = (P("seg", None, "slab", None), P("seg", None, None, "slab", None))
    return jax.shard_map(
        shards, mesh=mesh, in_specs=placed, out_specs=P("seg", None, "slab", None), check_vma=False
    )
```

profile of v0, /device:TPU:0, one launch (start us, length us, event | category | flops | bytes accessed | tf_op | source)
XLA Modules:
  0.0 402.6 jit_solution(13128962922173816920)
XLA Ops:
  8.0 3.8 multiply_subtract_fusion.3
  12.8 2.1 multiply_subtract_fusion.7
  15.8 1.9 multiply_subtract_fusion.11
  26.7 3.5 collective-permute-start.4
  30.2 16.2 %collective-permute-done.4 = f32[4,8,4096]{2,0,1:T(4,128)S(1)} collective-permute-done((f32[4,8,4096]{2,0,1:T(4,128)S(1)}, f32[4,8,4096]{2,0,1:T(4,128)S(1)}, u32[]{:S(2)}, u32[]{:S(2)}) %collective-permute-start.4) | collective-permute-done | bytes 524320 | tf_op jit(solution)/shard_map/ppermute | solution.py:25
  47.2 2.3 convolution_bitcast_fusion.4
  49.6 37.5 %psum.28 = f32[4,4]{0,1:T(4,128)S(1)} all-reduce(f32[4,4]{0,1:T(4,128)S(1)} %convolution_bitcast_fusion.4), channel_id=1, replica_groups=mesh['seg'=16,'slab'=2] {'seg','slab'}, use_global_device_ids=true, to_apply=%region_0.1 | all-reduce | flops 16 | bytes 128 | tf_op jit(solution)/shard_map/psum | solution.py:76
  102.4 2.5 fusion.24
  109.0 3.5 multiply_subtract_fusion.2
  113.5 2.1 multiply_subtract_fusion.6
  116.3 1.9 multiply_subtract_fusion.10
  121.6 1.7 multiply_subtract_fusion.18
  128.5 2.3 collective-permute-start.7
  130.8 15.3 %collective-permute-done.7 = f32[4,8,4096]{2,0,1:T(4,128)S(1)} collective-permute-done((f32[4,8,4096]{2,0,1:T(4,128)S(1)}, f32[4,8,4096]{2,0,1:T(4,128)S(1)}, u32[]{:S(2)}, u32[]{:S(2)}) %collective-permute-start.7) | collective-permute-done | bytes 524320 | tf_op jit(solution)/shard_map/ppermute | solution.py:25
  146.2 2.3 convolution_bitcast_fusion.3
  148.6 38.1 %psum.29 = f32[4,4]{0,1:T(4,128)S(1)} all-reduce(f32[4,4]{0,1:T(4,128)S(1)} %convolution_bitcast_fusion.3), channel_id=1, replica_groups=mesh['seg'=16,'slab'=2] {'seg','slab'}, use_global_device_ids=true, to_apply=%region_3.5 | all-reduce | flops 16 | bytes 128 | tf_op jit(solution)/shard_map/psum | solution.py:76
  207.9 3.5 multiply_subtract_fusion.1
  212.3 2.1 multiply_subtract_fusion.5
  215.2 1.9 multiply_subtract_fusion.9
  220.5 1.9 multiply_subtract_fusion.17
  228.1 2.3 collective-permute-start.10
  230.5 15.3 %collective-permute-done.10 = f32[4,8,4096]{2,0,1:T(4,128)S(1)} collective-permute-done((f32[4,8,4096]{2,0,1:T(4,128)S(1)}, f32[4,8,4096]{2,0,1:T(4,128)S(1)}, u32[]{:S(2)}, u32[]{:S(2)}) %collective-permute-start.10) | collective-permute-done | bytes 524320 | tf_op jit(solution)/shard_map/ppermute | solution.py:25
  245.9 2.3 convolution_bitcast_fusion.2
  248.2 37.4 %psum.30 = f32[4,4]{0,1:T(4,128)S(1)} all-reduce(f32[4,4]{0,1:T(4,128)S(1)} %convolution_bitcast_fusion.2), channel_id=1, replica_groups=mesh['seg'=16,'slab'=2] {'seg','slab'}, use_global_device_ids=true, to_apply=%region_4.6 | all-reduce | flops 16 | bytes 128 | tf_op jit(solution)/shard_map/psum | solution.py:76
  306.8 3.5 multiply_subtract_fusion
  311.3 2.1 multiply_subtract_fusion.4
  314.1 1.9 multiply_subtract_fusion.8
  319.4 1.6 multiply_subtract_fusion.16
  326.8 2.3 collective-permute-start.13
  329.1 15.3 %collective-permute-done.13 = f32[4,8,4096]{2,0,1:T(4,128)S(1)} collective-permute-done((f32[4,8,4096]{2,0,1:T(4,128)S(1)}, f32[4,8,4096]{2,0,1:T(4,128)S(1)}, u32[]{:S(2)}, u32[]{:S(2)}) %collective-permute-start.13) | collective-permute-done | bytes 524320 | tf_op jit(solution)/shard_map/ppermute | solution.py:25
  344.6 2.3 convolution_bitcast_fusion.1
  346.9 38.2 %psum.31 = f32[4,4]{0,1:T(4,128)S(1)} all-reduce(f32[4,4]{0,1:T(4,128)S(1)} %convolution_bitcast_fusion.1), channel_id=1, replica_groups=mesh['seg'=16,'slab'=2] {'seg','slab'}, use_global_device_ids=true, to_apply=%region_5.7 | all-reduce | flops 16 | bytes 128 | tf_op jit(solution)/shard_map/psum | solution.py:76
  (217 shorter events, 79.0 us)
Async XLA Ops:
  1.4 2.1 collective-permute-start.1
  1.9 2.3 collective-permute-start
  2.0 3.7 collective-permute-start.3
  2.5 4.8 %collective-permute-start.2 = (bf16[8,2,8,4096]{3,2,1,0:T(8,128)(2,1)}, bf16[8,2,8,4096]{3,2,1,0:T(8,128)(2,1)S(1)}, u32[]{:S(2)}, u32[]{:S(2)}) collective-permute-start(bf16[8,2,8,4096]{3,2,1,0:T(8,128)(2,1)} %bitcast.228), channel_id=1, source_target_pairs={{0,1},{1,0},{2,3},{3,2},{4,5},{5,4},{6,7},{7,6},{8,9},{9,8},{10,11... | collective-permute-start | bytes 3145736 | tf_op jit(solution)/shard_map/ppermute | solution.py:16
  4.8 2.4 copy-start.28
  18.5 1.6 copy-start.14
  18.5 1.6 copy-start.18
  23.0 100.8 %copy-start = (f32[12,4096]{1,0:T(8,128)}, f32[12,4096]{1,0:T(8,128)S(1)}, u32[]{:S(2)}) copy-start(f32[12,4096]{1,0:T(8,128)S(1)} %get-tuple-element.138) | copy-start | bytes 589828
  23.0 100.8 %copy-start.3 = (f32[12,4096]{1,0:T(8,128)}, f32[12,4096]{1,0:T(8,128)S(1)}, u32[]{:S(2)}) copy-start(f32[12,4096]{1,0:T(8,128)S(1)} %get-tuple-element.139) | copy-start | bytes 589828
  26.0 21.2 %copy-start.22 = (f32[1,4,8,4096]{3,2,1,0:T(8,128)S(1)}, f32[1,4,8,4096]{3,2,1,0:T(8,128)}, u32[]{:S(2)}) copy-start(f32[1,4,8,4096]{3,2,1,0:T(8,128)} %param.3) | copy-start | bytes 1572868
  26.7 19.7 %collective-permute-start.4 = (f32[4,8,4096]{2,0,1:T(4,128)S(1)}, f32[4,8,4096]{2,0,1:T(4,128)S(1)}, u32[]{:S(2)}, u32[]{:S(2)}) collective-permute-start(f32[4,8,4096]{2,0,1:T(4,128)S(1)} %multiply_subtract_fusion.31), channel_id=1, source_target_pairs={{30,0},{0,2},{2,4},{4,6},{6,8},{8,10},{10,12},{12,14},{14,16},{16,... | collective-permute-start | bytes 1572872 | tf_op jit(solution)/shard_map/ppermute | solution.py:25
  104.8 2.0 collective-permute-start.6
  104.9 2.6 collective-permute-start.5
  118.3 1.0 copy-start.15
  118.3 1.0 copy-start.19
  125.0 1.0 copy-start.11
  128.5 17.6 %collective-permute-start.7 = (f32[4,8,4096]{2,0,1:T(4,128)S(1)}, f32[4,8,4096]{2,0,1:T(4,128)S(1)}, u32[]{:S(2)}, u32[]{:S(2)}) collective-permute-start(f32[4,8,4096]{2,0,1:T(4,128)S(1)} %multiply_subtract_fusion.30), channel_id=1, source_target_pairs={{30,0},{0,2},{2,4},{4,6},{6,8},{8,10},{10,12},{12,14},{14,16},{16,... | collective-permute-start | bytes 1572872 | tf_op jit(solution)/shard_map/ppermute | solution.py:25
  203.7 2.0 collective-permute-start.9
  203.8 2.6 collective-permute-start.8
  217.2 1.0 copy-start.16
  217.2 1.0 copy-start.20
  222.5 1.0 copy-start.1
  222.5 1.0 copy-start.4
  224.6 1.0 copy-start.12
  228.1 17.6 %collective-permute-start.10 = (f32[4,8,4096]{2,0,1:T(4,128)S(1)}, f32[4,8,4096]{2,0,1:T(4,128)S(1)}, u32[]{:S(2)}, u32[]{:S(2)}) collective-permute-start(f32[4,8,4096]{2,0,1:T(4,128)S(1)} %multiply_subtract_fusion.29), channel_id=1, source_target_pairs={{30,0},{0,2},{2,4},{4,6},{6,8},{8,10},{10,12},{12,14},{14,16},{16,... | collective-permute-start | bytes 1572872 | tf_op jit(solution)/shard_map/ppermute | solution.py:25
  302.6 2.0 collective-permute-start.12
  302.7 2.6 collective-permute-start.11
  316.1 1.0 copy-start.17
  316.1 1.0 copy-start.21
  321.1 1.0 copy-start.5
  323.3 1.0 copy-start.13
  326.8 17.6 %collective-permute-start.13 = (f32[4,8,4096]{2,0,1:T(4,128)S(1)}, f32[4,8,4096]{2,0,1:T(4,128)S(1)}, u32[]{:S(2)}, u32[]{:S(2)}) collective-permute-start(f32[4,8,4096]{2,0,1:T(4,128)S(1)} %multiply_subtract_fusion.28), channel_id=1, source_target_pairs={{30,0},{0,2},{2,4},{4,6},{6,8},{8,10},{10,12},{12,14},{14,16},{16,... | collective-permute-start | bytes 1572872 | tf_op jit(solution)/shard_map/ppermute | solution.py:25
  (11 other events, 9.8 us)
where the time goes:
time: 407 us; the launch traced here: 403 us
  blocking collectives  151 us (37%)
  waiting for transfers between devices  71.7 us (18%)
  other arithmetic  65.1 us (16%)
  between operations  52.8 us (13%)
  local copies, waits for them, and re-layouts  33.8 us (8%)
  matrix products  14.7 us (4%)
  starting transfers between devices  13.3 us (3%)
    psum x4, blocking collectives, shards(): gram = lax.psum(local_gram, ('seg', 'slab'))  151 us
    ppermute x4, waiting for transfers between devices, shifted(): return lax.ppermute(block, axis, route)  62.1 us
    sub x32, other arithmetic, advance(): centre + 0.2 * (up + down + east + west - 4.0 * centre)  53.8 us
    slice x60, local copies, waits for them, and re-layouts, advance(): east = jnp.roll(centre, -1, 2)  21.5 us
    ppermute x4, starting transfers between devices, shifted(): return lax.ppermute(block, axis, route)  10.5 us
    dot_general x4, matrix products, shards(): jnp.einsum('ayx,byx->ab', residual, residual, precision=lax.Precision.HIG...  9.32 us
  transfers between devices with their start and end apart: 14, of which 13 were waited for; matrix products, arithmetic and copies ran while one was open for 0% of the time, Pallas kernels for 0%

commit v1 on v0

--- a/solution.py
+++ b/solution.py
@@ -73,7 +73,7 @@
         arrived = shifted(moved, "seg", 1)
         residual = arrived - vectors
         local_gram = jnp.einsum("ayx,byx->ab", residual, residual, precision=lax.Precision.HIGHEST)
-        gram = lax.psum(local_gram, ("seg", "slab"))
+        gram = lax.psum(lax.psum(local_gram, "slab"), "seg")
         inverse = lower_inverse(jnp.linalg.cholesky(gram))
         vectors = jnp.einsum("ab,byx->ayx", inverse, residual, precision=lax.Precision.HIGHEST)
     return vectors[None]

time: 407 us -> 411 us (level)
  blocking collectives: 151 us -> 158 us
    psum x4 -> x8, blocking collectives: 151 us -> 158 us  [shards(): gram = lax.psum(lax.psum(local_gram, 'slab'), 'seg')]
where the time goes in v1:
time: 411 us; the launch traced here: 408 us
  blocking collectives  158 us (38%)
  waiting for transfers between devices  74.3 us (18%)
  other arithmetic  64.9 us (16%)
  between operations  51.5 us (13%)
  local copies, waits for them, and re-layouts  33.8 us (8%)
  matrix products  14.7 us (4%)
  starting transfers between devices  10.8 us (3%)
    psum x8, blocking collectives, shards(): gram = lax.psum(lax.psum(local_gram, 'slab'), 'seg')  158 us
    ppermute x4, waiting for transfers between devices, shifted(): return lax.ppermute(block, axis, route)  64.6 us
    sub x32, other arithmetic, advance(): centre + 0.2 * (up + down + east + west - 4.0 * centre)  53.8 us
    slice x60, local copies, waits for them, and re-layouts, advance(): east = jnp.roll(centre, -1, 2)  21.5 us
    dot_general x4, matrix products, shards(): jnp.einsum('ayx,byx->ab', residual, residual, precision=lax.Precision.HIG...  9.32 us
  transfers between devices with their start and end apart: 14, of which 13 were waited for; matrix products, arithmetic and copies ran while one was open for 0% of the time, Pallas kernels for 0%

profile of v1, /device:TPU:0, one launch (start us, length us, event | category | flops | bytes accessed | tf_op | source)
XLA Modules:
  0.0 407.7 jit_solution(3839665061770412189)
XLA Ops:
  8.0 3.8 multiply_subtract_fusion.3
  12.8 2.1 multiply_subtract_fusion.7
  15.8 1.9 multiply_subtract_fusion.11
  26.7 3.5 collective-permute-start.4
  30.2 16.2 %collective-permute-done.4 = f32[4,8,4096]{2,0,1:T(4,128)S(1)} collective-permute-done((f32[4,8,4096]{2,0,1:T(4,128)S(1)}, f32[4,8,4096]{2,0,1:T(4,128)S(1)}, u32[]{:S(2)}, u32[]{:S(2)}) %collective-permute-start.4) | collective-permute-done | bytes 524320 | tf_op jit(solution)/shard_map/ppermute | solution.py:25
  47.2 2.3 convolution_bitcast_fusion.4
  49.6 2.5 psum.56
  52.0 38.3 %psum.57 = f32[4,4]{0,1:T(4,128)S(1)} all-reduce(f32[4,4]{0,1:T(4,128)S(1)} %psum.56), channel_id=1, replica_groups=mesh['seg'=16,'slab'=2] {'seg'}, use_global_device_ids=true, to_apply=%region_1.2 | all-reduce | flops 16 | bytes 128 | tf_op jit(solution)/shard_map/psum | solution.py:76
  105.4 2.5 fusion.24
  112.0 3.5 multiply_subtract_fusion.2
  116.5 2.1 multiply_subtract_fusion.6
  119.3 1.9 multiply_subtract_fusion.10
  131.8 17.3 %collective-permute-done.7 = f32[4,8,4096]{2,0,1:T(4,128)S(1)} collective-permute-done((f32[4,8,4096]{2,0,1:T(4,128)S(1)}, f32[4,8,4096]{2,0,1:T(4,128)S(1)}, u32[]{:S(2)}, u32[]{:S(2)}) %collective-permute-start.7) | collective-permute-done | bytes 524320 | tf_op jit(solution)/shard_map/ppermute | solution.py:25
  149.2 2.3 convolution_bitcast_fusion.3
  151.6 2.5 psum.58
  154.0 36.5 %psum.59 = f32[4,4]{0,1:T(4,128)S(1)} all-reduce(f32[4,4]{0,1:T(4,128)S(1)} %psum.58), channel_id=1, replica_groups=mesh['seg'=16,'slab'=2] {'seg'}, use_global_device_ids=true, to_apply=%region_5.7 | all-reduce | flops 16 | bytes 128 | tf_op jit(solution)/shard_map/psum | solution.py:76
  211.0 3.5 multiply_subtract_fusion.1
  215.4 2.1 multiply_subtract_fusion.5
  218.3 1.9 multiply_subtract_fusion.9
  223.5 1.9 multiply_subtract_fusion.17
  231.2 2.1 collective-permute-start.10
  233.3 15.6 %collective-permute-done.10 = f32[4,8,4096]{2,0,1:T(4,128)S(1)} collective-permute-done((f32[4,8,4096]{2,0,1:T(4,128)S(1)}, f32[4,8,4096]{2,0,1:T(4,128)S(1)}, u32[]{:S(2)}, u32[]{:S(2)}) %collective-permute-start.10) | collective-permute-done | bytes 524320 | tf_op jit(solution)/shard_map/ppermute | solution.py:25
  248.9 2.3 convolution_bitcast_fusion.2
  251.3 2.5 psum.60
  253.7 36.5 %psum.61 = f32[4,4]{0,1:T(4,128)S(1)} all-reduce(f32[4,4]{0,1:T(4,128)S(1)} %psum.60), channel_id=1, replica_groups=mesh['seg'=16,'slab'=2] {'seg'}, use_global_device_ids=true, to_apply=%region_7.9 | all-reduce | flops 16 | bytes 128 | tf_op jit(solution)/shard_map/psum | solution.py:76
  310.7 3.5 multiply_subtract_fusion
  315.1 2.1 multiply_subtract_fusion.4
  330.6 2.1 collective-permute-start.13
  332.7 15.6 %collective-permute-done.13 = f32[4,8,4096]{2,0,1:T(4,128)S(1)} collective-permute-done((f32[4,8,4096]{2,0,1:T(4,128)S(1)}, f32[4,8,4096]{2,0,1:T(4,128)S(1)}, u32[]{:S(2)}, u32[]{:S(2)}) %collective-permute-start.13) | collective-permute-done | bytes 524320 | tf_op jit(solution)/shard_map/ppermute | solution.py:25
  348.4 2.3 convolution_bitcast_fusion.1
  350.7 2.5 psum.62
  353.2 36.5 %psum.63 = f32[4,4]{0,1:T(4,128)S(1)} all-reduce(f32[4,4]{0,1:T(4,128)S(1)} %psum.62), channel_id=1, replica_groups=mesh['seg'=16,'slab'=2] {'seg'}, use_global_device_ids=true, to_apply=%region_9.11 | all-reduce | flops 16 | bytes 128 | tf_op jit(solution)/shard_map/psum | solution.py:76
  (221 shorter events, 84.3 us)
Async XLA Ops:
  1.4 2.1 collective-permute-start.1
  1.9 2.3 collective-permute-start
  2.0 3.7 collective-permute-start.3
  2.5 4.8 %collective-permute-start.2 = (bf16[8,2,8,4096]{3,2,1,0:T(8,128)(2,1)}, bf16[8,2,8,4096]{3,2,1,0:T(8,128)(2,1)S(1)}, u32[]{:S(2)}, u32[]{:S(2)}) collective-permute-start(bf16[8,2,8,4096]{3,2,1,0:T(8,128)(2,1)} %bitcast.228), channel_id=1, source_target_pairs={{0,1},{1,0},{2,3},{3,2},{4,5},{5,4},{6,7},{7,6},{8,9},{9,8},{10,11... | collective-permute-start | bytes 3145736 | tf_op jit(solution)/shard_map/ppermute | solution.py:16
  4.8 2.4 copy-start.28
  18.5 1.6 copy-start.14
  18.5 1.6 copy-start.18
  23.0 103.8 %copy-start = (f32[12,4096]{1,0:T(8,128)}, f32[12,4096]{1,0:T(8,128)S(1)}, u32[]{:S(2)}) copy-start(f32[12,4096]{1,0:T(8,128)S(1)} %get-tuple-element.138) | copy-start | bytes 589828
  23.0 103.8 %copy-start.3 = (f32[12,4096]{1,0:T(8,128)}, f32[12,4096]{1,0:T(8,128)S(1)}, u32[]{:S(2)}) copy-start(f32[12,4096]{1,0:T(8,128)S(1)} %get-tuple-element.139) | copy-start | bytes 589828
  26.0 21.2 %copy-start.22 = (f32[1,4,8,4096]{3,2,1,0:T(8,128)S(1)}, f32[1,4,8,4096]{3,2,1,0:T(8,128)}, u32[]{:S(2)}) copy-start(f32[1,4,8,4096]{3,2,1,0:T(8,128)} %param.3) | copy-start | bytes 1572868
  26.7 19.7 %collective-permute-start.4 = (f32[4,8,4096]{2,0,1:T(4,128)S(1)}, f32[4,8,4096]{2,0,1:T(4,128)S(1)}, u32[]{:S(2)}, u32[]{:S(2)}) collective-permute-start(f32[4,8,4096]{2,0,1:T(4,128)S(1)} %multiply_subtract_fusion.31), channel_id=1, source_target_pairs={{30,0},{0,2},{2,4},{4,6},{6,8},{8,10},{10,12},{12,14},{14,16},{16,... | collective-permute-start | bytes 1572872 | tf_op jit(solution)/shard_map/ppermute | solution.py:25
  107.8 2.0 collective-permute-start.6
  107.9 2.6 collective-permute-start.5
  121.3 1.0 copy-start.15
  121.3 1.0 copy-start.19
  128.0 1.0 copy-start.11
  131.5 17.6 %collective-permute-start.7 = (f32[4,8,4096]{2,0,1:T(4,128)S(1)}, f32[4,8,4096]{2,0,1:T(4,128)S(1)}, u32[]{:S(2)}, u32[]{:S(2)}) collective-permute-start(f32[4,8,4096]{2,0,1:T(4,128)S(1)} %multiply_subtract_fusion.30), channel_id=1, source_target_pairs={{30,0},{0,2},{2,4},{4,6},{6,8},{8,10},{10,12},{12,14},{14,16},{16,... | collective-permute-start | bytes 1572872 | tf_op jit(solution)/shard_map/ppermute | solution.py:25
  206.8 2.0 collective-permute-start.9
  206.8 2.6 collective-permute-start.8
  220.2 1.0 copy-start.16
  220.2 1.0 copy-start.20
  225.5 1.0 copy-start.1
  225.5 1.0 copy-start.4
  227.7 1.0 copy-start.12
  231.2 17.6 %collective-permute-start.10 = (f32[4,8,4096]{2,0,1:T(4,128)S(1)}, f32[4,8,4096]{2,0,1:T(4,128)S(1)}, u32[]{:S(2)}, u32[]{:S(2)}) collective-permute-start(f32[4,8,4096]{2,0,1:T(4,128)S(1)} %multiply_subtract_fusion.29), channel_id=1, source_target_pairs={{30,0},{0,2},{2,4},{4,6},{6,8},{8,10},{10,12},{12,14},{14,16},{16,... | collective-permute-start | bytes 1572872 | tf_op jit(solution)/shard_map/ppermute | solution.py:25
  306.5 2.0 collective-permute-start.12
  306.5 2.6 collective-permute-start.11
  319.9 1.0 copy-start.17
  319.9 1.0 copy-start.21
  325.0 1.0 copy-start.5
  327.1 1.0 copy-start.13
  330.6 17.6 %collective-permute-start.13 = (f32[4,8,4096]{2,0,1:T(4,128)S(1)}, f32[4,8,4096]{2,0,1:T(4,128)S(1)}, u32[]{:S(2)}, u32[]{:S(2)}) collective-permute-start(f32[4,8,4096]{2,0,1:T(4,128)S(1)} %multiply_subtract_fusion.28), channel_id=1, source_target_pairs={{30,0},{0,2},{2,4},{4,6},{6,8},{8,10},{10,12},{12,14},{14,16},{16,... | collective-permute-start | bytes 1572872 | tf_op jit(solution)/shard_map/ppermute | solution.py:25
  (11 other events, 9.8 us)
